TPU v7x, 16 devices: a 4x2x1 block of a 4x4x8 slice. The times are simulated.
16 devices in a mesh: dp: 2 (over y, z), ep: 8 (over x, core).
Axes of the slice: x: 4, y: 2, z: 1, core: 2. Of those that a mesh axis runs over, the one named last changes fastest.
The devices are a block of a 4x4x8 slice.
Arguments:
- x: bfloat16 [2, 8, 256, 2048], P('dp', 'ep'), parts along dimension 0
- expert: int32 [2, 8, 256, 8], P('dp', 'ep'), parts along dimension 0
- slot: int32 [2, 8, 256, 8], P('dp', 'ep'), parts along dimension 0
- gate: float32 [2, 8, 256, 8], P('dp', 'ep'), parts along dimension 0
- w_gate: bfloat16 [64, 2048, 1024], P('ep')
- w_up: bfloat16 [64, 2048, 1024], P('ep')
- w_down: bfloat16 [64, 1024, 2048], P('ep')
Outputs:
- y: bfloat16 [2, 8, 256, 2048], P('dp', 'ep'), parts along dimension 0
There are 2 independent parts. A program takes and returns all parts, laid end to end along the dimension named above; an argument that names none is the same for every part.
All inputs are finite; a program needn't handle non-finite values.
Results may differ from a plain program's by a relative error of at most 0.009.
Values are sent between devices in bfloat16 or wider.
A program may use at most 768 MiB of HBM per device.

v0:
```python
import jax
import jax.numpy as jnp
from jax import lax
from jax.sharding import NamedSharding, PartitionSpec as P


def einsum(form, a, b):
    return jnp.einsum(form, a.astype(jnp.float32), b.astype(jnp.float32))


def solution(mesh):
    def placed(v, *spec):
        return lax.with_sharding_constraint(v, NamedSharding(mesh, P(*spec)))

    def step(x, expert, slot, gate, w_gate, w_up, w_down):
        experts, (tokens, top) = w_gate.shape[0], expert.shape[2:]
        slots = 5 * tokens * top // (4 * experts)
        to_expert = jax.nn.one_hot(expert, experts, dtype=jnp.bfloat16)
        to_slot = jax.nn.one_hot(slot, slots, dtype=jnp.bfloat16)
        weighted = to_expert * gate[..., None].astype(jnp.bfloat16)
        dispatch = einsum("abtke,abtkc->abtec", to_expert, to_slot).astype(jnp.bfloat16)
        combine = einsum("abtke,abtkc->abtec", weighted, to_slot).astype(jnp.bfloat16)
        z = einsum("abtec,abtd->aebcd", dispatch, x).astype(jnp.bfloat16)
        z = placed(z, "dp", None, "ep", None, None)
        z = placed(z, "dp", "ep", None, None, None)
        h = jax.nn.silu(einsum("aebcd,edf->aebcf", z, w_gate))
        h = (h * einsum("aebcd,edf->aebcf", z, w_up)).astype(jnp.bfloat16)
        out = einsum("aebcf,efd->aebcd", h, w_down).astype(jnp.bfloat16)
        out = placed(out, "dp", "ep", None, None, None)
        out = placed(out, "dp", None, "ep", None, None)
        y = einsum("abtec,aebcd->abtd", combine, out)
        return y.astype(jnp.bfloat16)

    return step
```

profile of v0, /device:TPU:112, one launch (start us, length us, event | category | flops | bytes accessed | tf_op | source)
XLA Modules:
  0.0 342.4 jit_solution(16890154860497164166)
XLA Ops:
  0.0 0.0 copy-start
  0.0 0.9 copy.10
  0.9 0.8 copy.12
  1.7 3.6 %convolution_convert_fusion.1 = bf16[256,64,40]{1,2,0:T(8,128)(2,1)} fusion(s32[256,8]{1,0:T(8,128)S(1)} %copy.12, s32[256,8]{1,0:T(8,128)S(1)} %copy.10), kind=kOutput, calls=%fused_computation.23 | convolution fusion | flops 11354112 | bytes 1327104 | tf_op jit(solution)/abtke,abtkc->abtec/dot_general | solution.py:8
  5.4 5.6 %copy.13 = bf16[256,64,40]{0,2,1:T(8,128)(2,1)S(1)} copy(bf16[256,64,40]{1,2,0:T(8,128)(2,1)} %convolution_convert_fusion.1) | data formatting | bytes 2621440 | tf_op jit(solution)/convert_element_type | solution.py:21
  11.0 0.0 copy-done
  11.0 3.1 convolution_convert_fusion
  14.1 122.3 %all-to-all.4 = bf16[1,8,8,1,40,2048]{5,4,2,3,0,1:T(8,128)(2,1)} all-to-all(bf16[1,8,8,1,40,2048]{5,4,2,3,0,1:T(8,128)(2,1)S(1)} %bitcast.88), channel_id=1, replica_groups=mesh['dp'=2,'ep'=8] {'ep'}, dimensions={1} | all-to-all | bytes 20971520 | tf_op jit(solution)/sharding_constraint;jit(solution)/sharding_constraint | solution.py:13
  136.4 22.0 %fusion.2 = f32[8,8,40,1024]{3,2,1,0:T(8,128)} fusion(bf16[8,2048,1024]{2,1,0:T(8,128)(2,1)} %param.5, bf16[1,8,8,1,40,2048]{5,4,2,3,0,1:T(8,128)(2,1)} %all-to-all.4), kind=kOutput, calls=%fused_computation.2 | convolution fusion | flops 10737418240 | bytes 54525952 | tf_op jit(solution)/aebcd,edf->aebcf/dot_general | solution.py:8
  158.4 23.2 %fusion.6 = bf16[1,8,8,40,1024]{4,3,2,1,0:T(8,128)(2,1)} fusion(f32[8,8,40,1024]{3,2,1,0:T(8,128)} %fusion.2, bf16[8,2048,1024]{2,1,0:T(8,128)(2,1)} %param.4, bf16[1,8,8,1,40,2048]{5,4,2,3,0,1:T(8,128)(2,1)} %all-to-all.4), kind=kOutput, calls=%fused_computation.7 | convolution fusion | flops 10753146880 | bytes 59768832 | tf_op jit(solution)/aebcd,edf->aebcf/dot_general | solution.py:8
  181.6 20.5 %convert_bitcast_fusion = bf16[1,8,8,1,40,2048]{5,4,2,1,3,0:T(8,128)(2,1)} fusion(bf16[8,1024,2048]{2,1,0:T(8,128)(2,1)} %param.6, bf16[1,8,8,40,1024]{4,3,2,1,0:T(8,128)(2,1)} %fusion.6), kind=kOutput, calls=%fused_computation.15 | convolution fusion | flops 10742661120 | bytes 49283072 | tf_op jit(solution)/aebcf,efd->aebcd/dot_general | solution.py:8
  202.1 10.1 %copy.16 = bf16[1,8,8,1,40,2048]{5,4,1,3,0,2:T(8,128)(2,1)} copy(bf16[1,8,8,1,40,2048]{5,4,2,1,3,0:T(8,128)(2,1)} %convert_bitcast_fusion) | data formatting | bytes 20971520 | tf_op jit(solution)/sharding_constraint;jit(solution)/sharding_constraint | solution.py:13
  212.3 0.0 copy-start.2
  212.3 5.7 %all-to-all-start.1 = ((bf16[1,8,8,1,40,2048]{5,4,1,3,0,2:T(8,128)(2,1)}), bf16[1,8,8,1,40,2048]{5,4,1,3,0,2:T(8,128)(2,1)}, u32[]{:S(2)}, u32[]{:S(2)}) async-start(bf16[1,8,8,1,40,2048]{5,4,1,3,0,2:T(8,128)(2,1)} %copy.16), calls=%async_computation.1 | async-start | bytes 20971520 | tf_op jit(solution)/sharding_constraint;jit(solution)/sharding_constraint | solution.py:13
  218.0 0.0 copy-done.2
  218.0 0.1 copy.11
  218.1 0.0 copy-start.1
  218.1 4.3 %convolution_convert_fusion.2 = bf16[256,64,40]{1,2,0:T(8,128)(2,1)} fusion(s32[256,8]{1,0:T(8,128)S(1)} %copy.12, s32[256,8]{1,0:T(8,128)S(1)} %copy.10, bf16[256,8]{1,0:T(8,128)(2,1)S(1)} %copy.11), kind=kOutput, calls=%fused_computation.24 | convolution fusion | flops 11485184 | bytes 1331200 | tf_op jit(solution)/abtke,abtkc->abtec/dot_general | solution.py:8
  222.4 5.6 %copy.23 = bf16[256,64,40]{0,2,1:T(8,128)(2,1)S(1)} copy(bf16[256,64,40]{1,2,0:T(8,128)(2,1)} %convolution_convert_fusion.2) | data formatting | bytes 2621440 | tf_op jit(solution)/convert_element_type | solution.py:22
  228.1 106.5 %all-to-all-done.1 = bf16[1,8,8,1,40,2048]{5,4,1,3,0,2:T(8,128)(2,1)} async-done(((bf16[1,8,8,1,40,2048]{5,4,1,3,0,2:T(8,128)(2,1)}), bf16[1,8,8,1,40,2048]{5,4,1,3,0,2:T(8,128)(2,1)}, u32[]{:S(2)}, u32[]{:S(2)}) %all-to-all-start.1) | async-done | bytes 10485792 | tf_op jit(solution)/sharding_constraint;jit(solution)/sharding_constraint | solution.py:13
  334.6 7.8 %fusion.22 = bf16[1,1,256,2048]{3,2,1,0:T(8,128)(2,1)} fusion(bf16[256,64,40]{0,2,1:T(8,128)(2,1)S(1)} %copy.23, bf16[64,40,2048]{2,1,0:T(8,128)(2,1)} %bitcast.25), kind=kOutput, calls=%fused_computation.22 | convolution fusion | flops 2684878848 | bytes 12845056 | tf_op jit(solution)/abtec,aebcd->abtd/dot_general | solution.py:8
  342.4 0.0 copy-done.1
  (1 shorter events, 0.0 us)
Async XLA Ops:
  0.0 11.0 %copy-start = (bf16[1,1,256,2048]{3,2,1,0:T(8,128)(2,1)S(1)}, bf16[1,1,256,2048]{3,2,1,0:T(8,128)(2,1)}, u32[]{:S(2)}) copy-start(bf16[1,1,256,2048]{3,2,1,0:T(8,128)(2,1)} %param.3) | copy-start | bytes 3145732
  212.3 5.7 %copy-start.2 = (f32[1,1,256,8]{2,3,1,0:T(8,128)S(1)}, f32[1,1,256,8]{2,3,1,0:T(8,128)}, u32[]{:S(2)}) copy-start(f32[1,1,256,8]{2,3,1,0:T(8,128)} %param.1) | copy-start | bytes 24580
  212.3 122.3 %all-to-all-start.1 = ((bf16[1,8,8,1,40,2048]{5,4,1,3,0,2:T(8,128)(2,1)}), bf16[1,8,8,1,40,2048]{5,4,1,3,0,2:T(8,128)(2,1)}, u32[]{:S(2)}, u32[]{:S(2)}) async-start(bf16[1,8,8,1,40,2048]{5,4,1,3,0,2:T(8,128)(2,1)} %copy.16), calls=%async_computation.1 | async-start | bytes 20971520 | tf_op jit(solution)/sharding_constraint;jit(solution)/sharding_constraint | solution.py:13
  218.1 124.3 %copy-start.1 = (bf16[1,1,256,2048]{3,2,1,0:T(8,128)(2,1)S(1)}, bf16[1,1,256,2048]{3,2,1,0:T(8,128)(2,1)}, u32[]{:S(2)}) copy-start(bf16[1,1,256,2048]{3,2,1,0:T(8,128)(2,1)} %param.3) | copy-start | bytes 3145732
where the time goes:
time: 343 us; the launch traced here: 342 us
  blocking collectives  122 us (36%)
  waiting for transfers between devices  107 us (31%)
  matrix products  84.6 us (25%)
  local copies, waits for them, and re-layouts  23.2 us (7%)
  starting transfers between devices  5.68 us (2%)
    another operation x1, blocking collectives, placed(): return lax.with_sharding_constraint(v, NamedSharding(mesh, P(*spec)))  122 us
    another operation x1, waiting for transfers between devices, placed(): return lax.with_sharding_constraint(v, NamedSharding(mesh, P(*spec)))  107 us
    dot_general x7, matrix products, einsum(): return jnp.einsum(form, a.astype(jnp.float32), b.astype(jnp.float32))  84.6 us
    another operation x1, local copies, waits for them, and re-layouts, placed(): return lax.with_sharding_constraint(v, NamedSharding(mesh, P(*spec)))  10.1 us
  transfers between devices with their start and end apart: 1, of which 1 were waited for; matrix products, arithmetic and copies ran while one was open for 3% of the time, Pallas kernels for 0%

commit v1 on v0

v1 whole, which is shorter than its diff:
```python
import functools

import jax
import jax.numpy as jnp
from jax import lax
from jax.experimental import pallas as pl
from jax.experimental.pallas import tpu as pltpu
from jax.sharding import PartitionSpec as P

MESH = pl.DeviceIdType.MESH
F32, BF16 = jnp.float32, jnp.bfloat16
GROUPS = ((0, 1), (2, 3), (4, 5), (6,), (7,))
AHEAD = 2
RING = 4
RING2 = 8


def kernel(
    n, slots,
    x_hbm, ex, sl, ga, wg_hbm, wu_hbm, wd_hbm, y_hbm,
    xall, accg, accu, z, h, disp, comb, wgb, wub, wdb, outs, me_e, me_s, me_g, pr, r1, r2,
    x_sem, wg_sem, wu_sem, wd_sem, y_sem, ms_sem, mr_sem, as_sem, ar_sem, ss_sem, sr_sem,
):
    experts = wg_hbm.shape[0]
    tokens, model = x_hbm.shape
    ff = wg_hbm.shape[2]
    top = ex.shape[0]
    rows = experts * slots
    chunks, _, _, width = xall.shape
    half = tokens // 2
    chips = n // 2
    me = lax.axis_index("ep")
    chip, core = me // 2, me % 2
    other = 1 - core
    lchip, rchip, ochip = (chip + chips - 1) % chips, (chip + 1) % chips, (chip + 2) % chips
    left, right, opp, partner = 2 * lchip + core, 2 * rchip + core, 2 * ochip + core, 2 * chip + other

    def rcopy(src, dst, ssem, rsem, dev):
        return pltpu.make_async_remote_copy(
            src_ref=src, dst_ref=dst, send_sem=ssem, recv_sem=rsem,
            device_id={"ep": dev}, device_id_type=MESH,
        )

    def xload(j):
        return pltpu.make_async_copy(x_hbm.at[:, pl.ds(j * width, width)], xall.at[j, me], x_sem.at[j])

    for j in range(chunks):
        xload(j).start()

    def wload(g, e, slot):
        k0, kk = GROUPS[g][0] * width, len(GROUPS[g]) * width
        return [
            pltpu.make_async_copy(w.at[e, pl.ds(k0, kk), :], b.at[slot, pl.ds(0, kk), :], s.at[slot])
            for w, b, s in ((wg_hbm, wgb, wg_sem), (wu_hbm, wub, wu_sem))
        ]

    def dload(c, e, slot):
        return pltpu.make_async_copy(wd_hbm.at[e, :, pl.ds(c * width, width)], wdb.at[slot], wd_sem.at[slot])

    for e in range(RING):
        for c in wload(0, e, e):
            c.start()

    barrier = pltpu.get_barrier_semaphore()
    for o in range(1, n):
        pl.semaphore_signal(barrier, inc=1, device_id={"ep": (me + o) % n}, device_id_type=MESH)
    pl.semaphore_wait(barrier, n - 1)

    def own(j):
        return [
            rcopy(xall.at[j, me], xall.at[j, me], as_sem.at[0, j], ar_sem.at[0, j], right),
            rcopy(xall.at[j, me], xall.at[j, me], as_sem.at[1, j], ar_sem.at[1, j], left),
            rcopy(xall.at[j, me], xall.at[j, me], as_sem.at[2, j], ar_sem.at[4, j], partner),
        ]

    def forward(j):
        lo, hi = pl.ds(0, half), pl.ds(half, half)
        return [
            rcopy(xall.at[j, left, lo], xall.at[j, left, lo], as_sem.at[3, j], ar_sem.at[2, j], right),
            rcopy(xall.at[j, right, hi], xall.at[j, right, hi], as_sem.at[4, j], ar_sem.at[3, j], left),
            rcopy(xall.at[j, left], xall.at[j, left], as_sem.at[5, j], ar_sem.at[5, j], partner),
            rcopy(xall.at[j, right], xall.at[j, right], as_sem.at[6, j], ar_sem.at[6, j], partner),
        ]

    def across(j):
        return [rcopy(xall.at[j, opp], xall.at[j, opp], as_sem.at[7, j], ar_sem.at[7, j], partner)]

    def got(dst, sem):
        rcopy(dst, dst, sem, sem, partner).wait_recv()

    def send_own(j):
        xload(j).wait()
        for c in own(j):
            c.start()

    def step_a(j):
        got(xall.at[j, left], ar_sem.at[0, j])
        got(xall.at[j, right], ar_sem.at[1, j])
        for c in forward(j):
            c.start()
        if j + AHEAD < chunks:
            send_own(j + AHEAD)

    def step_b(j):
        got(xall.at[j, opp, pl.ds(0, half)], ar_sem.at[2, j])
        got(xall.at[j, opp, pl.ds(half, half)], ar_sem.at[3, j])
        for c in across(j):
            c.start()

    def step_c(j):
        for i, q in enumerate((chip, lchip, rchip, ochip)):
            got(xall.at[j, 2 * q + other], ar_sem.at[4 + i, j])

    for j in range(AHEAD):
        send_own(j)

    def meta(o):
        to = (me + o) % n
        return [
            rcopy(src, dst.at[me], ms_sem.at[i, o - 1], mr_sem.at[i, o - 1], to)
            for i, (src, dst) in enumerate(((ex, me_e), (sl, me_s), (ga, me_g)))
        ]

    for o in range(1, n):
        for c in meta(o):
            c.start()
    me_e[me] = ex[...]
    me_s[me] = sl[...]
    me_g[me] = ga[...]
    for e in range(RING2):
        dload(0, e, e).start()
    for o in range(1, n):
        source = (me + n - o) % n
        for i, dst in enumerate((me_e, me_s, me_g)):
            got(dst.at[source], mr_sem.at[i, o - 1])

    def tables(s, _):
        e, c, g = me_e[s], me_s[s], me_g[s]
        local = e - experts * me
        ok = (local >= 0) & (local < experts) & (c < slots)
        code = jnp.where(ok, local * slots + c, -1)
        for r0 in range(0, rows, 128):
            size = min(128, rows - r0)
            row = r0 + lax.broadcasted_iota(jnp.int32, (size, tokens), 0)
            w = jnp.zeros((size, tokens), F32)
            d = jnp.zeros((size, tokens), F32)
            for k in range(top):
                hit = row == code[k : k + 1, :]
                w = jnp.where(hit, g[k : k + 1, :], w)
                d = jnp.where(hit, 1.0, d)
            disp[s, r0 : r0 + size, :] = d.astype(BF16)
            comb[s, :, r0 : r0 + size] = w.T.astype(BF16)
        return _

    lax.fori_loop(0, n, tables, 0)

    def dispatch(j, k0):
        def pair(q, _):
            a = jnp.dot(disp[2 * q], xall[j, 2 * q], preferred_element_type=F32)
            b = jnp.dot(disp[2 * q + 1], xall[j, 2 * q + 1], preferred_element_type=F32)
            at = pl.ds(pl.multiple_of(q * 2 * slots, 16), 2 * slots)
            for e in range(experts):
                part = slice(e * slots, (e + 1) * slots)
                z[e, at, k0 : k0 + width] = jnp.concatenate([a[part], b[part]], 0).astype(BF16)
            return _

        lax.fori_loop(0, chips, pair, 0)

    def gemm1(g, e0, e1):
        kk = len(GROUPS[g]) * width
        first, last = g == 0, g == len(GROUPS) - 1

        def one(e, _):
            slot = e % RING
            for c in wload(g, e, slot):
                c.wait()
            lhs = z[e, :, :kk]
            for f0 in range(0, ff, width):
                f = slice(f0, f0 + width)
                gg = jnp.dot(lhs, wgb[slot, :kk, f], preferred_element_type=F32)
                uu = jnp.dot(lhs, wub[slot, :kk, f], preferred_element_type=F32)
                if not first:
                    gg += accg[e, :, f]
                    uu += accu[e, :, f]
                if last:
                    h[e, :, f] = (gg * jax.nn.sigmoid(gg) * uu).astype(BF16)
                else:
                    accg[e, :, f] = gg
                    accu[e, :, f] = uu
            if e1 + RING <= experts:
                for c in wload(g, e + RING, slot):
                    c.start()
            elif not last:
                for c in wload(g + 1, e + RING - experts, slot):
                    c.start()
            return _

        lax.fori_loop(e0, e1, one, 0)

    mid = experts // 2
    before = (
        lambda: (step_a(0), step_a(1), step_b(0), step_a(2), step_b(1), step_c(0), step_c(1)),
        lambda: (step_a(4), step_b(3), step_c(2), step_c(3)),
        lambda: (step_a(6), step_b(5), step_c(4), step_c(5)),
        lambda: (step_c(6),),
        lambda: (step_c(7),),
    )
    within = (
        lambda: (step_a(3), step_b(2)),
        lambda: (step_a(5), step_b(4)),
        lambda: (step_a(7), step_b(6)),
        lambda: (step_b(7),),
        lambda: (),
    )
    for g, js in enumerate(GROUPS):
        before[g]()
        for i, j in enumerate(js):
            dispatch(j, i * width)
        gemm1(g, 0, mid)
        within[g]()
        gemm1(g, mid, experts)

    for o in range(1, n):
        for c in meta(o):
            c.wait_send()
    for j in range(chunks):
        for c in own(j) + forward(j) + across(j):
            c.wait_send()

    keep = lambda c, q: accg.at[c, pl.ds(0, tokens), pl.ds(pl.multiple_of(q * width, width), width)]

    def die(c):
        return rcopy(xall.at[c, pl.ds(0, chips)], pr.at[c], ss_sem.at[0, c], sr_sem.at[0, c], partner)

    lo, hi = pl.ds(0, half), pl.ds(half, half)

    def far(c):
        return [
            rcopy(xall.at[c, chips, lo], r1.at[c, 0], ss_sem.at[1, c], sr_sem.at[1, c], right),
            rcopy(xall.at[c, chips, hi], r1.at[c, 1], ss_sem.at[2, c], sr_sem.at[2, c], left),
        ]

    def near(c):
        return [
            rcopy(xall.at[c, chips + 1, hi], r2.at[c, 0, hi], ss_sem.at[3, c], sr_sem.at[3, c], right),
            rcopy(xall.at[c, chips + 2, lo], r2.at[c, 1, lo], ss_sem.at[4, c], sr_sem.at[4, c], left),
        ]

    def merged(c):
        return [
            rcopy(xall.at[c, chips + 1, lo], r2.at[c, 0, lo], ss_sem.at[5, c], sr_sem.at[5, c], right),
            rcopy(xall.at[c, chips + 2, hi], r2.at[c, 1, hi], ss_sem.at[6, c], sr_sem.at[6, c], left),
        ]

    def store(c):
        return pltpu.make_async_copy(
            xall.at[c, chips + 3], y_hbm.at[:, pl.ds(pl.multiple_of(c * width, width), width)], y_sem.at[c]
        )

    def both(c, q, at):
        return keep(c, q)[at] + pr[c, q, at].astype(F32)

    def compute(c):
        def pair(i, _):
            pieces = []
            for b in range(2):
                e = 2 * i + b
                dload(c, e, e % RING2).wait()
                pieces.append(jnp.dot(h[e], wdb[e % RING2], preferred_element_type=F32))
            at = pl.ds(pl.multiple_of(i * 2 * slots, 16), 2 * slots)
            for s in range(n):
                part = slice(s * slots, (s + 1) * slots)
                outs[s, at, :] = jnp.concatenate([v[part] for v in pieces], 0).astype(BF16)

            @pl.when(c + 1 < chunks)
            def _next():
                for b in range(2):
                    e = 2 * i + b
                    dload(c + 1, e, e % RING2).start()

            return _

        lax.fori_loop(0, experts // 2, pair, 0)
        for q in range(chips):
            s = 2 * q + other
            xall[c, q] = jnp.dot(comb[s], outs[s], preferred_element_type=F32).astype(BF16)
        die(c).start()
        for q in range(chips):
            s = 2 * q + core
            keep(c, q)[...] = jnp.dot(comb[s], outs[s], preferred_element_type=F32)

    def stage1(c):
        die(c).wait_recv()
        xall[c, chips] = both(c, ochip, pl.ds(0, tokens)).astype(BF16)
        xall[c, chips + 1, hi] = both(c, rchip, hi).astype(BF16)
        xall[c, chips + 2, lo] = both(c, lchip, lo).astype(BF16)
        for k in far(c) + near(c):
            k.start()

    def stage2(c):
        for k in far(c):
            k.wait_recv()
        xall[c, chips + 1, lo] = (both(c, rchip, lo) + r1[c, 0].astype(F32)).astype(BF16)
        xall[c, chips + 2, hi] = (both(c, lchip, hi) + r1[c, 1].astype(F32)).astype(BF16)
        for k in merged(c):
            k.start()

    def stage3(c):
        for k in near(c) + merged(c):
            k.wait_recv()
        total = both(c, chip, pl.ds(0, tokens)) + r2[c, 0].astype(F32) + r2[c, 1].astype(F32)
        xall[c, chips + 3] = total.astype(BF16)
        store(c).start()

    def round_(t, _):
        for lag, stage in enumerate((compute, stage1, stage2, stage3)):
            pl.when((t >= lag) & (t < chunks + lag))(functools.partial(stage, t - lag))
        return _

    lax.fori_loop(0, chunks + 3, round_, 0)

    def drain(c, _):
        die(c).wait_send()
        for k in far(c) + near(c) + merged(c):
            k.wait_send()
        store(c).wait()
        return _

    lax.fori_loop(0, chunks, drain, 0)


def solution(mesh):
    n = mesh.shape["ep"]

    def local(x, expert, slot, gate, w_gate, w_up, w_down):
        tokens, model = x.shape[2:]
        top = expert.shape[3]
        experts, _, ff = w_gate.shape
        slots = 5 * tokens * top // (4 * experts * n)
        rows = experts * slots
        width = 256
        chunks = model // width
        flat = lambda v: v.reshape(tokens, top).T
        vmem = pltpu.VMEM
        dma = pltpu.SemaphoreType.DMA
        any_, inv = pl.BlockSpec(memory_space=pl.ANY), pl.BlockSpec(memory_space=pltpu.VMEM)
        flops = 6 * n * rows * model * ff
        y = pl.pallas_call(
            functools.partial(kernel, n, slots),
            out_shape=jax.ShapeDtypeStruct((tokens, model), BF16),
            in_specs=[any_, inv, inv, inv, any_, any_, any_],
            out_specs=any_,
            scratch_shapes=[
                vmem((chunks, n, tokens, width), BF16),
                vmem((experts, n * slots, ff), F32),
                vmem((experts, n * slots, ff), F32),
                vmem((experts, n * slots, 2 * width), BF16),
                vmem((experts, n * slots, ff), BF16),
                vmem((n, rows, tokens), BF16),
                vmem((n, tokens, rows), BF16),
                vmem((RING, 2 * width, ff), BF16),
                vmem((RING, 2 * width, ff), BF16),
                vmem((RING2, ff, width), BF16),
                vmem((n, rows, width), BF16),
                vmem((n, top, tokens), jnp.int32),
                vmem((n, top, tokens), jnp.int32),
                vmem((n, top, tokens), F32),
                vmem((chunks, n // 2, tokens, width), BF16),
                vmem((chunks, 2, tokens // 2, width), BF16),
                vmem((chunks, 2, tokens, width), BF16),
                dma((chunks,)),
                dma((RING,)),
                dma((RING,)),
                dma((RING2,)),
                dma((chunks,)),
                dma((3, n - 1)),
                dma((3, n - 1)),
                dma((8, chunks)),
                dma((8, chunks)),
                dma((7, chunks)),
                dma((7, chunks)),
            ],
            compiler_params=pltpu.CompilerParams(
                collective_id=0, has_side_effects=True, vmem_limit_bytes=67_000_000
            ),
            cost_estimate=pl.CostEstimate(
                flops=flops, bytes_accessed=6 * experts * model * ff, transcendentals=n * rows * ff
            ),
            name="moe",
        )(x.reshape(tokens, model), flat(expert), flat(slot), flat(gate), w_gate, w_up, w_down)
        return y.reshape(x.shape)

    token, weight = P("dp", "ep", None, None), P("ep", None, None)
    return jax.shard_map(
        local,
        mesh=mesh,
        in_specs=(token,) * 4 + (weight,) * 3,
        out_specs=token,
        check_vma=False,
    )
```

time: 343 us -> 130 us (0.38)
  Pallas kernels: 0 us -> 127 us
  blocking collectives: 122 us -> 0 us
  waiting for transfers between devices: 107 us -> 0 us
  matrix products: 84.6 us -> 0 us
  local copies, waits for them, and re-layouts: 23.2 us -> 2.3 us
  starting transfers between devices: 5.68 us -> 0 us
    pallas_call x0 -> x1, Pallas kernels: none -> 127 us  [local(): pl.pallas_call(functools.partial(kernel, n, slots), out_shape=jax.ShapeDt...]
    another operation x1 -> x0, blocking collectives: 122 us -> none  [placed(): return lax.with_sharding_constraint(v, NamedSharding(mesh, P(*spec)))]
    another operation x1 -> x0, waiting for transfers between devices: 107 us -> none  [placed(): return lax.with_sharding_constraint(v, NamedSharding(mesh, P(*spec)))]
    dot_general x7 -> x0, matrix products: 84.6 us -> none  [einsum(): return jnp.einsum(form, a.astype(jnp.float32), b.astype(jnp.float32))]
    convert_element_type x3 -> x0, local copies, waits for them, and re-layouts: 11.4 us -> none  [the longest x1 5.62 us: step(): einsum('abtke,abtkc->abtec', to_expert, to_slot).astype(jnp.bfloat16)]
    another operation x1 -> x0, local copies, waits for them, and re-layouts: 10.1 us -> none  [placed(): return lax.with_sharding_constraint(v, NamedSharding(mesh, P(*spec)))]
    another operation x1 -> x0, starting transfers between devices: 5.68 us -> none  [placed(): return lax.with_sharding_constraint(v, NamedSharding(mesh, P(*spec)))]
  transfers between devices with their start and end apart: 1 -> 0, of which waited for: 1 -> 0; matrix products, arithmetic and copies ran while one was open for 3% -> 0% of each run, Pallas kernels for 0% -> 0%
where the time goes in v1:
time: 130 us
  Pallas kernels  127 us (98%)
  local copies, waits for them, and re-layouts  2.3 us (2%)
    pallas_call x1, Pallas kernels, local(): pl.pallas_call(functools.partial(kernel, n, slots), out_shape=jax.ShapeDt...  127 us

profile of v1, /device:TPU:112, one launch (start us, length us, event | category | flops | bytes accessed | tf_op | source)
XLA Modules:
  0.0 129.8 jit_solution(15154431386407276268)
XLA Ops:
  0.0 127.5 %moe.1 = bf16[256,2048]{1,0:T(8,128)(2,1)} custom-call(bf16[256,2048]{1,0:T(8,128)(2,1)} %bitcast.12, s32[8,256]{1,0:T(8,128)} %bitcast.13, s32[8,256]{1,0:T(8,128)} %bitcast.14, f32[8,256]{1,0:T(8,128)} %bitcast.15, bf16[8,2048,1024]{2,1,0:T(8,128)(2,1)} %wg_hbm.1, bf16[8,2048,1024]{2,1,0:T(8,128)(2,1)} %wu_hbm.1, bf16[8,1024,2048]{2,1,0:T(8,128)(2,1)} %wd_hbm.1), custom_call_target="tpu_custom_call" | custom-call | flops 32212254720 | bytes 100663296 | tf_op jit(solution)/shard_map/moe/pallas_call | solution.py:348
  127.5 2.3 %copy.9 = bf16[1,1,256,2048]{3,2,1,0:T(8,128)(2,1)} copy(bf16[1,1,256,2048]{3,2,1,0:T(8,128)(2,1)} %bitcast.11) | data formatting | bytes 2097152

commit v2 on v1

v2 whole, which is shorter than its diff:
```python
import functools

import jax
import jax.numpy as jnp
from jax import lax
from jax.experimental import pallas as pl
from jax.experimental.pallas import tpu as pltpu
from jax.sharding import PartitionSpec as P

MESH = pl.DeviceIdType.MESH
F32, BF16 = jnp.float32, jnp.bfloat16
GROUPS = ((0,), (1, 2), (3, 4), (5, 6), (7,))
DOWN = (1, 2, 2, 2, 1)
AHEAD = 2
RING = 4
PAD = 128


def kernel(
    n, slots, width,
    x_hbm, ex, sl, ga, wg_hbm, wu_hbm, wd_hbm, y_hbm,
    xall, accg, accu, z, h, disp, comb, wgb, wub, wdb, me_c, me_g, pr, r1, r2,
    x_sem, wg_sem, wu_sem, wd_sem, y_sem, ms_sem, mr_sem, as_sem, ar_sem, ss_sem, sr_sem,
):
    experts = wg_hbm.shape[0]
    tokens = x_hbm.shape[0]
    ff = wg_hbm.shape[2]
    top = ex.shape[0]
    rows = experts * slots
    chunks = xall.shape[0]
    half = tokens // 2
    chips = n // 2
    me = lax.axis_index("ep")
    chip, core = me // 2, me % 2
    other = 1 - core
    lchip, rchip, ochip = (chip + chips - 1) % chips, (chip + 1) % chips, (chip + 2) % chips
    left, right, opp, partner = 2 * lchip + core, 2 * rchip + core, 2 * ochip + core, 2 * chip + other
    others = tuple(2 * q + other for q in (chip, lchip, rchip, ochip))

    def rcopy(src, dst, ssem, rsem, dev):
        return pltpu.make_async_remote_copy(
            src_ref=src, dst_ref=dst, send_sem=ssem, recv_sem=rsem,
            device_id={"ep": dev}, device_id_type=MESH,
        )

    def go(copies):
        for c in copies:
            c.start()

    def got(dst, sem):
        rcopy(dst, dst, sem, sem, partner).wait_recv()

    def xload(j):
        return pltpu.make_async_copy(x_hbm.at[:, pl.ds(j * width, width)], xall.at[j, me], x_sem.at[j])

    go([xload(j) for j in range(chunks)])

    def wload(g, e, slot):
        k0, kk = GROUPS[g][0] * width, len(GROUPS[g]) * width
        return [
            pltpu.make_async_copy(
                w.at[e, pl.ds(k0, kk), :], b.at[slot, pl.ds(0, kk), pl.ds(0, ff)], s.at[slot]
            )
            for w, b, s in ((wg_hbm, wgb, wg_sem), (wu_hbm, wub, wu_sem))
        ]

    def dload(c0, nc, e, slot):
        cols = pl.ds(pl.multiple_of(c0 * width, width), nc * width)
        return pltpu.make_async_copy(
            wd_hbm.at[e, :, cols], wdb.at[slot, :, pl.ds(0, nc * width)], wd_sem.at[slot]
        )

    for e in range(RING):
        go(wload(0, e, e))
    go([dload(0, DOWN[0], e, e) for e in range(RING)])

    barrier = pltpu.get_barrier_semaphore()
    for p in (left, right, partner):
        pl.semaphore_signal(barrier, inc=1, device_id={"ep": p}, device_id_type=MESH)
    me_c[me] = jnp.where(sl[...] < slots, ex[...] * slots + sl[...], -1)
    me_g[me] = ga[...]
    pl.semaphore_wait(barrier, 3)

    def table(i, r, s, dev):
        return [
            rcopy(t.at[s], t.at[s], ms_sem.at[k, i], mr_sem.at[k, r], dev) for k, t in enumerate((me_c, me_g))
        ]

    def tgot(r, s):
        for k, t in enumerate((me_c, me_g)):
            got(t.at[s], mr_sem.at[k, r])

    t_own = table(0, 0, me, right) + table(1, 1, me, left) + table(2, 4, me, partner)
    t_next = table(3, 2, left, right) + table(4, 5, left, partner) + table(5, 6, right, partner)
    t_last = table(6, 7, opp, partner)

    def own(j):
        return [
            rcopy(xall.at[j, me], xall.at[j, me], as_sem.at[0, j], ar_sem.at[0, j], right),
            rcopy(xall.at[j, me], xall.at[j, me], as_sem.at[1, j], ar_sem.at[1, j], left),
            rcopy(xall.at[j, me], xall.at[j, me], as_sem.at[2, j], ar_sem.at[4, j], partner),
        ]

    lo, hi = pl.ds(0, half), pl.ds(half, half)

    def forward(j):
        return [
            rcopy(xall.at[j, left, lo], xall.at[j, left, lo], as_sem.at[3, j], ar_sem.at[2, j], right),
            rcopy(xall.at[j, right, hi], xall.at[j, right, hi], as_sem.at[4, j], ar_sem.at[3, j], left),
            rcopy(xall.at[j, left], xall.at[j, left], as_sem.at[5, j], ar_sem.at[5, j], partner),
            rcopy(xall.at[j, right], xall.at[j, right], as_sem.at[6, j], ar_sem.at[6, j], partner),
        ]

    def across(j):
        return [rcopy(xall.at[j, opp], xall.at[j, opp], as_sem.at[7, j], ar_sem.at[7, j], partner)]

    def send_own(j):
        xload(j).wait()
        go(own(j))

    def step_a(j):
        got(xall.at[j, left], ar_sem.at[0, j])
        got(xall.at[j, right], ar_sem.at[1, j])
        go(forward(j))
        if j + AHEAD < chunks:
            send_own(j + AHEAD)

    def step_b(j):
        got(xall.at[j, opp, lo], ar_sem.at[2, j])
        got(xall.at[j, opp, hi], ar_sem.at[3, j])
        go(across(j))

    def step_c(j):
        for i, s in enumerate(others):
            got(xall.at[j, s], ar_sem.at[4 + i, j])

    A, B, C = (functools.partial(functools.partial, f) for f in (step_a, step_b, step_c))

    go(t_own)
    for j in range(AHEAD):
        send_own(j)
    tgot(0, left)
    tgot(1, right)
    go(t_next)
    tgot(2, opp)
    go(t_last)
    step_a(0)
    for i, s in enumerate(others):
        tgot(4 + i, s)

    def tables(s, _):
        code, g = me_c[s] - rows * me, me_g[s]
        for r0 in range(0, rows, 128):
            size = min(128, rows - r0)
            row = r0 + lax.broadcasted_iota(jnp.int32, (size, tokens), 0)
            w = jnp.zeros((size, tokens), F32)
            d = jnp.zeros((size, tokens), F32)
            for k in range(top):
                hit = row == code[k : k + 1, :]
                w = jnp.where(hit, g[k : k + 1, :], w)
                d = jnp.where(hit, 1.0, d)
            disp[s, r0 : r0 + size, :] = d.astype(BF16)
            comb[s, :, r0 : r0 + size] = w.T.astype(BF16)
        return _

    lax.fori_loop(0, n - 2, tables, 0)
    step_a(1)
    lax.fori_loop(n - 2, n, tables, 0)

    def dispatch(j, k0):
        for q in range(chips):
            a = jnp.dot(disp[2 * q], xall[j, 2 * q], preferred_element_type=F32)
            b = jnp.dot(disp[2 * q + 1], xall[j, 2 * q + 1], preferred_element_type=F32)
            at = slice(q * 2 * slots, (q + 1) * 2 * slots)
            for e in range(experts):
                part = slice(e * slots, (e + 1) * slots)
                z[e, at, k0 : k0 + width] = jnp.concatenate([a[part], b[part]], 0).astype(BF16)

    def gemm1(g, hooks):
        kk = len(GROUPS[g]) * width
        first, last = g == 0, g == len(GROUPS) - 1

        def one(e, _):
            for at, hook in hooks:
                pl.when(e == at)(hook)
            slot = e % RING
            for c in wload(g, e, slot):
                c.wait()
            lhs = z[e, :, :kk]
            for f0 in range(0, ff, width):
                f = slice(f0, f0 + width)
                gg = jnp.dot(lhs, wgb[slot, :kk, f], preferred_element_type=F32)
                uu = jnp.dot(lhs, wub[slot, :kk, f], preferred_element_type=F32)
                if not first:
                    gg += accg[e, :, f]
                    uu += accu[e, :, f]
                if last:
                    h[e, :, f] = (gg * jax.nn.sigmoid(gg) * uu).astype(BF16)
                else:
                    accg[e, :, f] = gg
                    accu[e, :, f] = uu
            pl.when(e + RING < experts)(lambda: go(wload(g, e + RING, slot)))
            if not last:
                pl.when(e + RING >= experts)(lambda: go(wload(g + 1, e + RING - experts, slot)))
            return _

        lax.fori_loop(0, experts, one, 0)

    before = (
        (B(0), C(0)),
        (A(3), B(2), C(1), C(2)),
        (A(5), B(4), C(3), C(4)),
        (A(7), B(6), C(5), C(6)),
        (C(7),),
    )
    within = (
        ((3, A(2)), (6, B(1))),
        ((2, A(4)), (4, B(3))),
        ((2, A(6)), (4, B(5))),
        ((2, B(7)),),
        (),
    )
    for g, js in enumerate(GROUPS):
        for f in before[g]:
            f()
        for i, j in enumerate(js):
            dispatch(j, i * width)
        gemm1(g, within[g])

    for c in t_own + t_next + t_last:
        c.wait_send()
    for j in range(chunks):
        for c in own(j) + forward(j) + across(j):
            c.wait_send()

    keep = lambda c, q: accg.at[c, pl.ds(0, tokens), pl.ds(pl.multiple_of(q * width, width), width)]

    def die(c):
        return rcopy(xall.at[c, pl.ds(0, chips)], pr.at[c], ss_sem.at[0, c], sr_sem.at[0, c], partner)

    def far(c):
        return [
            rcopy(xall.at[c, chips, lo], r1.at[c, 0], ss_sem.at[1, c], sr_sem.at[1, c], right),
            rcopy(xall.at[c, chips, hi], r1.at[c, 1], ss_sem.at[2, c], sr_sem.at[2, c], left),
        ]

    def near(c):
        return [
            rcopy(xall.at[c, chips + 1, hi], r2.at[c, 0, hi], ss_sem.at[3, c], sr_sem.at[3, c], right),
            rcopy(xall.at[c, chips + 2, lo], r2.at[c, 1, lo], ss_sem.at[4, c], sr_sem.at[4, c], left),
        ]

    def merged(c):
        return [
            rcopy(xall.at[c, chips + 1, lo], r2.at[c, 0, lo], ss_sem.at[5, c], sr_sem.at[5, c], right),
            rcopy(xall.at[c, chips + 2, hi], r2.at[c, 1, hi], ss_sem.at[6, c], sr_sem.at[6, c], left),
        ]

    def store(c):
        return pltpu.make_async_copy(
            xall.at[c, chips + 3], y_hbm.at[:, pl.ds(pl.multiple_of(c * width, width), width)], y_sem.at[c]
        )

    def both(c, q, at):
        return keep(c, q)[at] + pr[c, q, at].astype(F32)

    def stage1(c):
        die(c).wait_recv()
        xall[c, chips] = both(c, ochip, pl.ds(0, tokens)).astype(BF16)
        xall[c, chips + 1, hi] = both(c, rchip, hi).astype(BF16)
        xall[c, chips + 2, lo] = both(c, lchip, lo).astype(BF16)
        go(far(c) + near(c))

    def stage2(c):
        for k in far(c):
            k.wait_recv()
        xall[c, chips + 1, lo] = (both(c, rchip, lo) + r1[c, 0].astype(F32)).astype(BF16)
        xall[c, chips + 2, hi] = (both(c, lchip, hi) + r1[c, 1].astype(F32)).astype(BF16)
        go(merged(c))

    def stage3(c):
        for k in near(c) + merged(c):
            k.wait_recv()
        total = both(c, chip, pl.ds(0, tokens)) + r2[c, 0].astype(F32) + r2[c, 1].astype(F32)
        xall[c, chips + 3] = total.astype(BF16)
        store(c).start()

    def down(c0, nc, after, hooks):
        cols = nc * width

        def pair(i, _):
            for at, hook in hooks:
                pl.when(i == at)(hook)
            pieces = []
            for b in range(2):
                slot = (2 * i + b) % RING
                dload(c0, nc, 2 * i + b, slot).wait()
                pieces.append(
                    jnp.dot(h[2 * i + b, :, :ff], wdb[slot, :, :cols], preferred_element_type=F32)
                )
            at = pl.ds(pl.multiple_of(i * 2 * slots, 16), 2 * slots)
            for s in range(n):
                part = slice(s * slots, (s + 1) * slots)
                z[s, at, :cols] = jnp.concatenate([v[part] for v in pieces], 0).astype(BF16)
            for b in range(2):
                e = 2 * i + b + RING
                pl.when(e < experts)(lambda: dload(c0, nc, e, e % RING).start())
                pl.when(e >= experts)(lambda: after(e - experts, e % RING))
            return _

        lax.fori_loop(0, experts // 2, pair, 0)
        for k in range(nc):
            col = slice(k * width, (k + 1) * width)
            for q in range(chips):
                s = 2 * q + other
                xall[c0 + k, q] = jnp.dot(comb[s], z[s, :, col], preferred_element_type=F32).astype(BF16)
            die(c0 + k).start()
        for k in range(nc):
            col = slice(k * width, (k + 1) * width)
            for q in range(chips):
                s = 2 * q + core
                keep(c0 + k, q)[...] = jnp.dot(comb[s], z[s, :, col], preferred_element_type=F32)

    def stages(*todo):
        for f, c in todo:
            f(c)

    down(0, 1, lambda e, slot: dload(1, 2, e, slot).start(), ())

    def middle(r, _):
        c = 2 * r - 1
        more = r < 3

        def after(e, slot):
            pl.when(more)(lambda: dload(c + 2, 2, e, slot).start())
            pl.when(jnp.logical_not(more))(lambda: dload(chunks - 1, 1, e, slot).start())

        def one():
            pl.when(r > 1)(lambda: stage1(c - 2))
            stage1(c - 1)

        def two():
            pl.when(r > 1)(lambda: stage2(c - 2))

        down(c, 2, after, ((1, one), (3, two)))
        stage2(c - 1)
        pl.when(r > 1)(lambda: stages((stage3, c - 3), (stage3, c - 2)))
        return _

    lax.fori_loop(1, 4, middle, 0)
    c = chunks - 1
    down(
        c, 1, lambda e, slot: None,
        ((1, lambda: stages((stage1, c - 2), (stage1, c - 1))), (3, lambda: stages((stage2, c - 2)))),
    )
    stages((stage1, c), (stage2, c - 1), (stage3, c - 3), (stage2, c), (stage3, c - 2), (stage3, c - 1), (stage3, c))

    def drain(c, _):
        die(c).wait_send()
        for k in far(c) + near(c) + merged(c):
            k.wait_send()
        store(c).wait()
        return _

    lax.fori_loop(0, chunks, drain, 0)


def solution(mesh):
    n = mesh.shape["ep"]

    def local(x, expert, slot, gate, w_gate, w_up, w_down):
        tokens, model = x.shape[2:]
        top = expert.shape[3]
        experts, _, ff = w_gate.shape
        slots = 5 * tokens * top // (4 * experts * n)
        rows = experts * slots
        width = 256
        chunks = model // width
        flat = lambda v: v.reshape(tokens, top).T
        vmem = pltpu.VMEM
        dma = pltpu.SemaphoreType.DMA
        any_, inv = pl.BlockSpec(memory_space=pl.ANY), pl.BlockSpec(memory_space=pltpu.VMEM)
        flops = 6 * n * rows * model * ff
        y = pl.pallas_call(
            functools.partial(kernel, n, slots, width),
            out_shape=jax.ShapeDtypeStruct((tokens, model), BF16),
            in_specs=[any_, inv, inv, inv, any_, any_, any_],
            out_specs=any_,
            scratch_shapes=[
                vmem((chunks, n, tokens, width), BF16),
                vmem((experts, n * slots, ff + PAD), F32),
                vmem((experts, n * slots, ff + PAD), F32),
                vmem((n, rows, 2 * width + PAD), BF16),
                vmem((experts, n * slots, ff + PAD), BF16),
                vmem((n, rows, tokens), BF16),
                vmem((n, tokens, rows), BF16),
                vmem((RING, 2 * width, ff + PAD), BF16),
                vmem((RING, 2 * width, ff + PAD), BF16),
                vmem((RING, ff, 2 * width + PAD), BF16),
                vmem((n, top, tokens), jnp.int32),
                vmem((n, top, tokens), F32),
                vmem((chunks, n // 2, tokens, width), BF16),
                vmem((chunks, 2, tokens // 2, width), BF16),
                vmem((chunks, 2, tokens, width), BF16),
                dma((chunks,)),
                dma((RING,)),
                dma((RING,)),
                dma((RING,)),
                dma((chunks,)),
                dma((2, 7)),
                dma((2, 8)),
                dma((8, chunks)),
                dma((8, chunks)),
                dma((7, chunks)),
                dma((7, chunks)),
            ],
            compiler_params=pltpu.CompilerParams(
                collective_id=0, has_side_effects=True, vmem_limit_bytes=67_000_000
            ),
            cost_estimate=pl.CostEstimate(
                flops=flops, bytes_accessed=6 * experts * model * ff, transcendentals=n * rows * ff
            ),
            name="moe",
        )(x.reshape(tokens, model), flat(expert), flat(slot), flat(gate), w_gate, w_up, w_down)
        return y.reshape(x.shape)

    token, weight = P("dp", "ep", None, None), P("ep", None, None)
    return jax.shard_map(
        local,
        mesh=mesh,
        in_specs=(token,) * 4 + (weight,) * 3,
        out_specs=token,
        check_vma=False,
    )
```

time: 130 us -> 113 us (0.87)
  Pallas kernels: 127 us -> 109 us
    pallas_call x1, Pallas kernels: 127 us -> 109 us  [local(): pl.pallas_call(functools.partial(kernel, n, slots, width), out_shape=jax....]
where the time goes in v2:
time: 113 us; the launch traced here: 112 us
  Pallas kernels  109 us (96%)
  local copies, waits for them, and re-layouts  2.3 us (2%)
    pallas_call x1, Pallas kernels, local(): pl.pallas_call(functools.partial(kernel, n, slots, width), out_shape=jax....  109 us
    unnamed x1, local copies, waits for them, and re-layouts  2.3 us

profile of v2, /device:TPU:112, one launch (start us, length us, event | category | flops | bytes accessed | tf_op | source)
XLA Modules:
  0.0 111.7 jit_solution(7590782065979651283)
XLA Ops:
  0.0 109.4 %moe.1 = bf16[256,2048]{1,0:T(8,128)(2,1)} custom-call(bf16[256,2048]{1,0:T(8,128)(2,1)} %bitcast.12, s32[8,256]{1,0:T(8,128)} %bitcast.13, s32[8,256]{1,0:T(8,128)} %bitcast.14, f32[8,256]{1,0:T(8,128)} %bitcast.15, bf16[8,2048,1024]{2,1,0:T(8,128)(2,1)} %wg_hbm.1, bf16[8,2048,1024]{2,1,0:T(8,128)(2,1)} %wu_hbm.1, bf16[8,1024,2048]{2,1,0:T(8,128)(2,1)} %wd_hbm.1), custom_call_target="tpu_custom_call" | custom-call | flops 32212254720 | bytes 100663296 | tf_op jit(solution)/shard_map/moe/pallas_call | solution.py:384
  109.4 2.3 %copy.9 = bf16[1,1,256,2048]{3,2,1,0:T(8,128)(2,1)} copy(bf16[1,1,256,2048]{3,2,1,0:T(8,128)(2,1)} %bitcast.11) | data formatting | bytes 2097152

commit v3 on v2

--- a/solution.py
+++ b/solution.py
@@ -9,11 +9,9 @@
 
 MESH = pl.DeviceIdType.MESH
 F32, BF16 = jnp.float32, jnp.bfloat16
-GROUPS = ((0,), (1, 2), (3, 4), (5, 6), (7,))
-DOWN = (1, 2, 2, 2, 1)
+GROUPS = ((0,), (1,), (2,), (3,), (4,), (5,), (6, 7))
 AHEAD = 2
 RING = 4
-PAD = 128
 
 
 def kernel(
@@ -64,15 +62,13 @@
             for w, b, s in ((wg_hbm, wgb, wg_sem), (wu_hbm, wub, wu_sem))
         ]
 
-    def dload(c0, nc, e, slot):
-        cols = pl.ds(pl.multiple_of(c0 * width, width), nc * width)
-        return pltpu.make_async_copy(
-            wd_hbm.at[e, :, cols], wdb.at[slot, :, pl.ds(0, nc * width)], wd_sem.at[slot]
-        )
+    def dload(r, e):
+        cols = pl.ds(pl.multiple_of(r * 2 * width, width), 2 * width)
+        return pltpu.make_async_copy(wd_hbm.at[e, :, cols], wdb.at[e], wd_sem.at[e])
 
     for e in range(RING):
         go(wload(0, e, e))
-    go([dload(0, DOWN[0], e, e) for e in range(RING)])
+    go([dload(0, e) for e in range(experts)])
 
     barrier = pltpu.get_barrier_semaphore()
     for p in (left, right, partner):
@@ -206,18 +202,14 @@
 
         lax.fori_loop(0, experts, one, 0)
 
-    before = (
-        (B(0), C(0)),
-        (A(3), B(2), C(1), C(2)),
-        (A(5), B(4), C(3), C(4)),
-        (A(7), B(6), C(5), C(6)),
-        (C(7),),
-    )
+    before = ((B(0), C(0)), (C(1),), (C(2),), (C(3),), (C(4),), (C(5),), (C(6), C(7)))
     within = (
-        ((3, A(2)), (6, B(1))),
-        ((2, A(4)), (4, B(3))),
-        ((2, A(6)), (4, B(5))),
-        ((2, B(7)),),
+        ((2, A(2)), (5, B(1))),
+        ((1, A(3)), (4, B(2))),
+        ((1, A(4)), (3, B(3))),
+        ((0, A(5)), (2, B(4)), (7, A(6))),
+        ((1, B(5)), (6, A(7))),
+        ((0, B(6)), (3, B(7))),
         (),
     )
     for g, js in enumerate(GROUPS):
@@ -285,75 +277,48 @@
         xall[c, chips + 3] = total.astype(BF16)
         store(c).start()
 
-    def down(c0, nc, after, hooks):
-        cols = nc * width
-
-        def pair(i, _):
-            for at, hook in hooks:
-                pl.when(i == at)(hook)
-            pieces = []
-            for b in range(2):
-                slot = (2 * i + b) % RING
-                dload(c0, nc, 2 * i + b, slot).wait()
-                pieces.append(
-                    jnp.dot(h[2 * i + b, :, :ff], wdb[slot, :, :cols], preferred_element_type=F32)
-                )
-            at = pl.ds(pl.multiple_of(i * 2 * slots, 16), 2 * slots)
+    def down(r, k, within, last):
+        c = 2 * r + k
+        col = slice(k * width, (k + 1) * width)
+        for i in range(experts // 2):
+            if i % 2 == 0 and k == 0:
+                for e in range(2 * i, 2 * i + 4):
+                    dload(r, e).wait()
+            pieces = [
+                jnp.dot(h[e], wdb[e, :, col], preferred_element_type=F32) for e in (2 * i, 2 * i + 1)
+            ]
+            at = slice(i * 2 * slots, (i + 1) * 2 * slots)
             for s in range(n):
                 part = slice(s * slots, (s + 1) * slots)
-                z[s, at, :cols] = jnp.concatenate([v[part] for v in pieces], 0).astype(BF16)
-            for b in range(2):
-                e = 2 * i + b + RING
-                pl.when(e < experts)(lambda: dload(c0, nc, e, e % RING).start())
-                pl.when(e >= experts)(lambda: after(e - experts, e % RING))
-            return _
-
-        lax.fori_loop(0, experts // 2, pair, 0)
-        for k in range(nc):
-            col = slice(k * width, (k + 1) * width)
-            for q in range(chips):
-                s = 2 * q + other
-                xall[c0 + k, q] = jnp.dot(comb[s], z[s, :, col], preferred_element_type=F32).astype(BF16)
-            die(c0 + k).start()
-        for k in range(nc):
-            col = slice(k * width, (k + 1) * width)
-            for q in range(chips):
-                s = 2 * q + core
-                keep(c0 + k, q)[...] = jnp.dot(comb[s], z[s, :, col], preferred_element_type=F32)
-
-    def stages(*todo):
-        for f, c in todo:
-            f(c)
-
-    down(0, 1, lambda e, slot: dload(1, 2, e, slot).start(), ())
-
-    def middle(r, _):
-        c = 2 * r - 1
-        more = r < 3
-
-        def after(e, slot):
-            pl.when(more)(lambda: dload(c + 2, 2, e, slot).start())
-            pl.when(jnp.logical_not(more))(lambda: dload(chunks - 1, 1, e, slot).start())
-
-        def one():
-            pl.when(r > 1)(lambda: stage1(c - 2))
-            stage1(c - 1)
-
-        def two():
-            pl.when(r > 1)(lambda: stage2(c - 2))
-
-        down(c, 2, after, ((1, one), (3, two)))
-        stage2(c - 1)
-        pl.when(r > 1)(lambda: stages((stage3, c - 3), (stage3, c - 2)))
+                z[s, at, :width] = jnp.concatenate([v[part] for v in pieces], 0).astype(BF16)
+            if i % 2:
+                if k == 1:
+                    pl.when(r + 1 < chunks // 2)(lambda: go([dload(r + 1, e) for e in range(2 * i - 2, 2 * i + 2)]))
+                (within if i == 1 else last)(c)
+        for q in range(chips):
+            s = 2 * q + other
+            xall[c, q] = jnp.dot(comb[s], z[s, :, :width], preferred_element_type=F32).astype(BF16)
+        die(c).start()
+        for q in range(chips):
+            s = 2 * q + core
+            keep(c, q)[...] = jnp.dot(comb[s], z[s, :, :width], preferred_element_type=F32)
+
+    def round_(r, _):
+        def within(c):
+            pl.when(c >= 1)(lambda: stage1(c - 1))
+
+        def last(c):
+            pl.when(c >= 2)(lambda: stage2(c - 2))
+            pl.when(c >= 4)(lambda: stage3(c - 4))
+
+        down(r, 0, within, last)
+        down(r, 1, within, last)
         return _
 
-    lax.fori_loop(1, 4, middle, 0)
+    lax.fori_loop(0, chunks // 2, round_, 0)
     c = chunks - 1
-    down(
-        c, 1, lambda e, slot: None,
-        ((1, lambda: stages((stage1, c - 2), (stage1, c - 1))), (3, lambda: stages((stage2, c - 2)))),
-    )
-    stages((stage1, c), (stage2, c - 1), (stage3, c - 3), (stage2, c), (stage3, c - 2), (stage3, c - 1), (stage3, c))
+    for f, k in ((stage1, 0), (stage2, 1), (stage3, 3), (stage2, 0), (stage3, 2), (stage3, 1), (stage3, 0)):
+        f(c - k)
 
     def drain(c, _):
         die(c).wait_send()
@@ -388,15 +353,15 @@
             out_specs=any_,
             scratch_shapes=[
                 vmem((chunks, n, tokens, width), BF16),
-                vmem((experts, n * slots, ff + PAD), F32),
-                vmem((experts, n * slots, ff + PAD), F32),
-                vmem((n, rows, 2 * width + PAD), BF16),
-                vmem((experts, n * slots, ff + PAD), BF16),
+                vmem((experts, n * slots, ff), F32),
+                vmem((experts, n * slots, ff), F32),
+                vmem((n, rows, 2 * width), BF16),
+                vmem((experts, n * slots, ff), BF16),
                 vmem((n, rows, tokens), BF16),
                 vmem((n, tokens, rows), BF16),
-                vmem((RING, 2 * width, ff + PAD), BF16),
-                vmem((RING, 2 * width, ff + PAD), BF16),
-                vmem((RING, ff, 2 * width + PAD), BF16),
+                vmem((RING, 2 * width, ff), BF16),
+                vmem((RING, 2 * width, ff), BF16),
+                vmem((experts, ff, 2 * width), BF16),
                 vmem((n, top, tokens), jnp.int32),
                 vmem((n, top, tokens), F32),
                 vmem((chunks, n // 2, tokens, width), BF16),
@@ -405,7 +370,7 @@
                 dma((chunks,)),
                 dma((RING,)),
                 dma((RING,)),
-                dma((RING,)),
+                dma((experts,)),
                 dma((chunks,)),
                 dma((2, 7)),
                 dma((2, 8)),

time: 113 us -> 104 us (0.920)
  Pallas kernels: 109 us -> 101 us
    pallas_call x1, Pallas kernels: 109 us -> 101 us  [local(): pl.pallas_call(functools.partial(kernel, n, slots, width), out_shape=jax....]
where the time goes in v3:
time: 104 us; the launch traced here: 103 us
  Pallas kernels  101 us (97%)
  local copies, waits for them, and re-layouts  2.3 us (2%)
    pallas_call x1, Pallas kernels, local(): pl.pallas_call(functools.partial(kernel, n, slots, width), out_shape=jax....  101 us
    unnamed x1, local copies, waits for them, and re-layouts  2.3 us

profile of v3, /device:TPU:112, one launch (start us, length us, event | category | flops | bytes accessed | tf_op | source)
XLA Modules:
  0.0 103.3 jit_solution(2914913102998971446)
XLA Ops:
  0.0 101.0 %moe.1 = bf16[256,2048]{1,0:T(8,128)(2,1)} custom-call(bf16[256,2048]{1,0:T(8,128)(2,1)} %bitcast.12, s32[8,256]{1,0:T(8,128)} %bitcast.13, s32[8,256]{1,0:T(8,128)} %bitcast.14, f32[8,256]{1,0:T(8,128)} %bitcast.15, bf16[8,2048,1024]{2,1,0:T(8,128)(2,1)} %wg_hbm.1, bf16[8,2048,1024]{2,1,0:T(8,128)(2,1)} %wu_hbm.1, bf16[8,1024,2048]{2,1,0:T(8,128)(2,1)} %wd_hbm.1), custom_call_target="tpu_custom_call" | custom-call | flops 32212254720 | bytes 100663296 | tf_op jit(solution)/shard_map/moe/pallas_call | solution.py:349
  101.0 2.3 %copy.9 = bf16[1,1,256,2048]{3,2,1,0:T(8,128)(2,1)} copy(bf16[1,1,256,2048]{3,2,1,0:T(8,128)(2,1)} %bitcast.11) | data formatting | bytes 2097152

commit v4 on v3

--- a/solution.py
+++ b/solution.py
@@ -9,7 +9,7 @@
 
 MESH = pl.DeviceIdType.MESH
 F32, BF16 = jnp.float32, jnp.bfloat16
-GROUPS = ((0,), (1,), (2,), (3,), (4,), (5,), (6, 7))
+GROUPS = ((0,), (1,), (2,), (3,), (4,), (5,), (6,), (7,))
 AHEAD = 2
 RING = 4
 
@@ -130,7 +130,7 @@
         for i, s in enumerate(others):
             got(xall.at[j, s], ar_sem.at[4 + i, j])
 
-    A, B, C = (functools.partial(functools.partial, f) for f in (step_a, step_b, step_c))
+    A, B = (functools.partial(functools.partial, f) for f in (step_a, step_b))
 
     go(t_own)
     for j in range(AHEAD):
@@ -176,48 +176,45 @@
         kk = len(GROUPS[g]) * width
         first, last = g == 0, g == len(GROUPS) - 1
 
-        def one(e, _):
+        def pair(p, _):
             for at, hook in hooks:
-                pl.when(e == at)(hook)
-            slot = e % RING
-            for c in wload(g, e, slot):
-                c.wait()
-            lhs = z[e, :, :kk]
-            for f0 in range(0, ff, width):
-                f = slice(f0, f0 + width)
-                gg = jnp.dot(lhs, wgb[slot, :kk, f], preferred_element_type=F32)
-                uu = jnp.dot(lhs, wub[slot, :kk, f], preferred_element_type=F32)
-                if not first:
-                    gg += accg[e, :, f]
-                    uu += accu[e, :, f]
-                if last:
-                    h[e, :, f] = (gg * jax.nn.sigmoid(gg) * uu).astype(BF16)
-                else:
-                    accg[e, :, f] = gg
-                    accu[e, :, f] = uu
-            pl.when(e + RING < experts)(lambda: go(wload(g, e + RING, slot)))
-            if not last:
-                pl.when(e + RING >= experts)(lambda: go(wload(g + 1, e + RING - experts, slot)))
+                pl.when(p == at)(hook)
+            es = (2 * p, 2 * p + 1)
+            for e in es:
+                for c in wload(g, e, e % RING):
+                    c.wait()
+            for e in es:
+                lhs = z[e, :, :kk]
+                for f0 in range(0, ff, width):
+                    f = slice(f0, f0 + width)
+                    gg = jnp.dot(lhs, wgb[e % RING, :kk, f], preferred_element_type=F32)
+                    uu = jnp.dot(lhs, wub[e % RING, :kk, f], preferred_element_type=F32)
+                    if not first:
+                        gg += accg[e, :, f]
+                        uu += accu[e, :, f]
+                    if last:
+                        h[e, :, f] = (gg * jax.nn.sigmoid(gg) * uu).astype(BF16)
+                    else:
+                        accg[e, :, f] = gg
+                        accu[e, :, f] = uu
+            for e in es:
+                pl.when(e + RING < experts)(lambda: go(wload(g, e + RING, e % RING)))
+                if not last:
+                    pl.when(e + RING >= experts)(lambda: go(wload(g + 1, e + RING - experts, e % RING)))
             return _
 
-        lax.fori_loop(0, experts, one, 0)
-
-    before = ((B(0), C(0)), (C(1),), (C(2),), (C(3),), (C(4),), (C(5),), (C(6), C(7)))
-    within = (
-        ((2, A(2)), (5, B(1))),
-        ((1, A(3)), (4, B(2))),
-        ((1, A(4)), (3, B(3))),
-        ((0, A(5)), (2, B(4)), (7, A(6))),
-        ((1, B(5)), (6, A(7))),
-        ((0, B(6)), (3, B(7))),
-        (),
-    )
+        lax.fori_loop(0, experts // 2, pair, 0)
+
+    def within(j):
+        return [(at, f(k)) for at, f, k in ((1, A, j + 2), (3, B, j + 1)) if k < chunks]
+
     for g, js in enumerate(GROUPS):
-        for f in before[g]:
-            f()
         for i, j in enumerate(js):
+            if j == 0:
+                step_b(0)
+            step_c(j)
             dispatch(j, i * width)
-        gemm1(g, within[g])
+        gemm1(g, within(js[0]))
 
     for c in t_own + t_next + t_last:
         c.wait_send()
@@ -355,12 +352,12 @@
                 vmem((chunks, n, tokens, width), BF16),
                 vmem((experts, n * slots, ff), F32),
                 vmem((experts, n * slots, ff), F32),
-                vmem((n, rows, 2 * width), BF16),
+                vmem((n, rows, width), BF16),
                 vmem((experts, n * slots, ff), BF16),
                 vmem((n, rows, tokens), BF16),
                 vmem((n, tokens, rows), BF16),
-                vmem((RING, 2 * width, ff), BF16),
-                vmem((RING, 2 * width, ff), BF16),
+                vmem((RING, width, ff), BF16),
+                vmem((RING, width, ff), BF16),
                 vmem((experts, ff, 2 * width), BF16),
                 vmem((n, top, tokens), jnp.int32),
                 vmem((n, top, tokens), F32),

time: 104 us -> 103 us (level)
  no operation moved by 1% of the time
where the time goes in v4:
time: 103 us; the launch traced here: 102 us
  Pallas kernels  100 us (97%)
  local copies, waits for them, and re-layouts  2.3 us (2%)
    pallas_call x1, Pallas kernels, local(): pl.pallas_call(functools.partial(kernel, n, slots, width), out_shape=jax....  100 us
    unnamed x1, local copies, waits for them, and re-layouts  2.3 us

profile of v4, /device:TPU:112, one launch (start us, length us, event | category | flops | bytes accessed | tf_op | source)
XLA Modules:
  0.0 102.4 jit_solution(6966692409823424482)
XLA Ops:
  0.0 100.1 %moe.1 = bf16[256,2048]{1,0:T(8,128)(2,1)} custom-call(bf16[256,2048]{1,0:T(8,128)(2,1)} %bitcast.12, s32[8,256]{1,0:T(8,128)} %bitcast.13, s32[8,256]{1,0:T(8,128)} %bitcast.14, f32[8,256]{1,0:T(8,128)} %bitcast.15, bf16[8,2048,1024]{2,1,0:T(8,128)(2,1)} %wg_hbm.1, bf16[8,2048,1024]{2,1,0:T(8,128)(2,1)} %wu_hbm.1, bf16[8,1024,2048]{2,1,0:T(8,128)(2,1)} %wd_hbm.1), custom_call_target="tpu_custom_call" | custom-call | flops 32212254720 | bytes 100663296 | tf_op jit(solution)/shard_map/moe/pallas_call | solution.py:346
  100.1 2.3 %copy.9 = bf16[1,1,256,2048]{3,2,1,0:T(8,128)(2,1)} copy(bf16[1,1,256,2048]{3,2,1,0:T(8,128)(2,1)} %bitcast.11) | data formatting | bytes 2097152

commit v5 on v4

--- a/solution.py
+++ b/solution.py
@@ -206,7 +206,7 @@
         lax.fori_loop(0, experts // 2, pair, 0)
 
     def within(j):
-        return [(at, f(k)) for at, f, k in ((1, A, j + 2), (3, B, j + 1)) if k < chunks]
+        return [(at, f(k)) for at, f, k in ((1, A, j + 2), (2, B, j + 1)) if k < chunks]
 
     for g, js in enumerate(GROUPS):
         for i, j in enumerate(js):

time: 103 us -> 103 us (level)
  no operation moved by 1% of the time
where the time goes in v5:
time: 103 us; the launch traced here: 102 us
  Pallas kernels  99.8 us (97%)
  local copies, waits for them, and re-layouts  2.3 us (2%)
    pallas_call x1, Pallas kernels, local(): pl.pallas_call(functools.partial(kernel, n, slots, width), out_shape=jax....  99.8 us
    unnamed x1, local copies, waits for them, and re-layouts  2.3 us

profile of v5, /device:TPU:112, one launch (start us, length us, event | category | flops | bytes accessed | tf_op | source)
XLA Modules:
  0.0 102.1 jit_solution(12977695215525606298)
XLA Ops:
  0.0 99.8 %moe.1 = bf16[256,2048]{1,0:T(8,128)(2,1)} custom-call(bf16[256,2048]{1,0:T(8,128)(2,1)} %bitcast.12, s32[8,256]{1,0:T(8,128)} %bitcast.13, s32[8,256]{1,0:T(8,128)} %bitcast.14, f32[8,256]{1,0:T(8,128)} %bitcast.15, bf16[8,2048,1024]{2,1,0:T(8,128)(2,1)} %wg_hbm.1, bf16[8,2048,1024]{2,1,0:T(8,128)(2,1)} %wu_hbm.1, bf16[8,1024,2048]{2,1,0:T(8,128)(2,1)} %wd_hbm.1), custom_call_target="tpu_custom_call" | custom-call | flops 32212254720 | bytes 100663296 | tf_op jit(solution)/shard_map/moe/pallas_call | solution.py:346
  99.8 2.3 %copy.9 = bf16[1,1,256,2048]{3,2,1,0:T(8,128)(2,1)} copy(bf16[1,1,256,2048]{3,2,1,0:T(8,128)(2,1)} %bitcast.11) | data formatting | bytes 2097152

commit v6 on v5

--- a/solution.py
+++ b/solution.py
@@ -11,7 +11,6 @@
 F32, BF16 = jnp.float32, jnp.bfloat16
 GROUPS = ((0,), (1,), (2,), (3,), (4,), (5,), (6,), (7,))
 AHEAD = 2
-RING = 4
 
 
 def kernel(
@@ -53,11 +52,11 @@
 
     go([xload(j) for j in range(chunks)])
 
-    def wload(g, e, slot):
+    def wload(g, e):
         k0, kk = GROUPS[g][0] * width, len(GROUPS[g]) * width
         return [
             pltpu.make_async_copy(
-                w.at[e, pl.ds(k0, kk), :], b.at[slot, pl.ds(0, kk), pl.ds(0, ff)], s.at[slot]
+                w.at[e, pl.ds(k0, kk), :], b.at[e, pl.ds(0, kk), :], s.at[e]
             )
             for w, b, s in ((wg_hbm, wgb, wg_sem), (wu_hbm, wub, wu_sem))
         ]
@@ -66,8 +65,8 @@
         cols = pl.ds(pl.multiple_of(r * 2 * width, width), 2 * width)
         return pltpu.make_async_copy(wd_hbm.at[e, :, cols], wdb.at[e], wd_sem.at[e])
 
-    for e in range(RING):
-        go(wload(0, e, e))
+    for e in range(experts):
+        go(wload(0, e))
     go([dload(0, e) for e in range(experts)])
 
     barrier = pltpu.get_barrier_semaphore()
@@ -181,14 +180,14 @@
                 pl.when(p == at)(hook)
             es = (2 * p, 2 * p + 1)
             for e in es:
-                for c in wload(g, e, e % RING):
+                for c in wload(g, e):
                     c.wait()
             for e in es:
                 lhs = z[e, :, :kk]
                 for f0 in range(0, ff, width):
                     f = slice(f0, f0 + width)
-                    gg = jnp.dot(lhs, wgb[e % RING, :kk, f], preferred_element_type=F32)
-                    uu = jnp.dot(lhs, wub[e % RING, :kk, f], preferred_element_type=F32)
+                    gg = jnp.dot(lhs, wgb[e, :kk, f], preferred_element_type=F32)
+                    uu = jnp.dot(lhs, wub[e, :kk, f], preferred_element_type=F32)
                     if not first:
                         gg += accg[e, :, f]
                         uu += accu[e, :, f]
@@ -197,10 +196,9 @@
                     else:
                         accg[e, :, f] = gg
                         accu[e, :, f] = uu
-            for e in es:
-                pl.when(e + RING < experts)(lambda: go(wload(g, e + RING, e % RING)))
-                if not last:
-                    pl.when(e + RING >= experts)(lambda: go(wload(g + 1, e + RING - experts, e % RING)))
+            if not last:
+                for e in es:
+                    go(wload(g + 1, e))
             return _
 
         lax.fori_loop(0, experts // 2, pair, 0)
@@ -356,8 +354,8 @@
                 vmem((experts, n * slots, ff), BF16),
                 vmem((n, rows, tokens), BF16),
                 vmem((n, tokens, rows), BF16),
-                vmem((RING, width, ff), BF16),
-                vmem((RING, width, ff), BF16),
+                vmem((experts, width, ff), BF16),
+                vmem((experts, width, ff), BF16),
                 vmem((experts, ff, 2 * width), BF16),
                 vmem((n, top, tokens), jnp.int32),
                 vmem((n, top, tokens), F32),
@@ -365,8 +363,8 @@
                 vmem((chunks, 2, tokens // 2, width), BF16),
                 vmem((chunks, 2, tokens, width), BF16),
                 dma((chunks,)),
-                dma((RING,)),
-                dma((RING,)),
+                dma((experts,)),
+                dma((experts,)),
                 dma((experts,)),
                 dma((chunks,)),
                 dma((2, 7)),

time: 103 us -> 98.5 us (0.956)
  Pallas kernels: 99.8 us -> 96 us
    pallas_call x1, Pallas kernels: 99.8 us -> 96 us  [local(): pl.pallas_call(functools.partial(kernel, n, slots, width), out_shape=jax....]
where the time goes in v6:
time: 98.5 us; the launch traced here: 98.3 us
  Pallas kernels  96 us (97%)
  local copies, waits for them, and re-layouts  2.3 us (2%)
    pallas_call x1, Pallas kernels, local(): pl.pallas_call(functools.partial(kernel, n, slots, width), out_shape=jax....  96 us
    unnamed x1, local copies, waits for them, and re-layouts  2.3 us

profile of v6, /device:TPU:112, one launch (start us, length us, event | category | flops | bytes accessed | tf_op | source)
XLA Modules:
  0.0 98.3 jit_solution(7318912109016001871)
XLA Ops:
  0.0 96.0 %moe.1 = bf16[256,2048]{1,0:T(8,128)(2,1)} custom-call(bf16[256,2048]{1,0:T(8,128)(2,1)} %bitcast.12, s32[8,256]{1,0:T(8,128)} %bitcast.13, s32[8,256]{1,0:T(8,128)} %bitcast.14, f32[8,256]{1,0:T(8,128)} %bitcast.15, bf16[8,2048,1024]{2,1,0:T(8,128)(2,1)} %wg_hbm.1, bf16[8,2048,1024]{2,1,0:T(8,128)(2,1)} %wu_hbm.1, bf16[8,1024,2048]{2,1,0:T(8,128)(2,1)} %wd_hbm.1), custom_call_target="tpu_custom_call" | custom-call | flops 32212254720 | bytes 100663296 | tf_op jit(solution)/shard_map/moe/pallas_call | solution.py:344
  96.0 2.3 %copy.9 = bf16[1,1,256,2048]{3,2,1,0:T(8,128)(2,1)} copy(bf16[1,1,256,2048]{3,2,1,0:T(8,128)(2,1)} %bitcast.11) | data formatting | bytes 2097152

commit v7 on v6

--- a/solution.py
+++ b/solution.py
@@ -10,6 +10,7 @@
 MESH = pl.DeviceIdType.MESH
 F32, BF16 = jnp.float32, jnp.bfloat16
 GROUPS = ((0,), (1,), (2,), (3,), (4,), (5,), (6,), (7,))
+STEP = 4
 AHEAD = 2
 
 
@@ -178,7 +179,7 @@
         def pair(p, _):
             for at, hook in hooks:
                 pl.when(p == at)(hook)
-            es = (2 * p, 2 * p + 1)
+            es = [STEP * p + i for i in range(STEP)]
             for e in es:
                 for c in wload(g, e):
                     c.wait()
@@ -201,10 +202,10 @@
                     go(wload(g + 1, e))
             return _
 
-        lax.fori_loop(0, experts // 2, pair, 0)
+        lax.fori_loop(0, experts // STEP, pair, 0)
 
     def within(j):
-        return [(at, f(k)) for at, f, k in ((1, A, j + 2), (2, B, j + 1)) if k < chunks]
+        return [(at, f(k)) for at, f, k in ((1, A, j + 2), (1, B, j + 1)) if k < chunks]
 
     for g, js in enumerate(GROUPS):
         for i, j in enumerate(js):

time: 98.5 us -> 97 us (0.985)
  Pallas kernels: 96 us -> 94.5 us
    pallas_call x1, Pallas kernels: 96 us -> 94.5 us  [local(): pl.pallas_call(functools.partial(kernel, n, slots, width), out_shape=jax....]
where the time goes in v7:
time: 97 us; the launch traced here: 96.8 us
  Pallas kernels  94.5 us (97%)
  local copies, waits for them, and re-layouts  2.3 us (2%)
    pallas_call x1, Pallas kernels, local(): pl.pallas_call(functools.partial(kernel, n, slots, width), out_shape=jax....  94.5 us
    unnamed x1, local copies, waits for them, and re-layouts  2.3 us

profile of v7, /device:TPU:112, one launch (start us, length us, event | category | flops | bytes accessed | tf_op | source)
XLA Modules:
  0.0 96.8 jit_solution(16039174765820377347)
XLA Ops:
  0.0 94.5 %moe.1 = bf16[256,2048]{1,0:T(8,128)(2,1)} custom-call(bf16[256,2048]{1,0:T(8,128)(2,1)} %bitcast.12, s32[8,256]{1,0:T(8,128)} %bitcast.13, s32[8,256]{1,0:T(8,128)} %bitcast.14, f32[8,256]{1,0:T(8,128)} %bitcast.15, bf16[8,2048,1024]{2,1,0:T(8,128)(2,1)} %wg_hbm.1, bf16[8,2048,1024]{2,1,0:T(8,128)(2,1)} %wu_hbm.1, bf16[8,1024,2048]{2,1,0:T(8,128)(2,1)} %wd_hbm.1), custom_call_target="tpu_custom_call" | custom-call | flops 32212254720 | bytes 100663296 | tf_op jit(solution)/shard_map/moe/pallas_call | solution.py:345
  94.5 2.3 %copy.9 = bf16[1,1,256,2048]{3,2,1,0:T(8,128)(2,1)} copy(bf16[1,1,256,2048]{3,2,1,0:T(8,128)(2,1)} %bitcast.11) | data formatting | bytes 2097152

commit v8 on v7

--- a/solution.py
+++ b/solution.py
@@ -90,38 +90,41 @@
     t_next = table(3, 2, left, right) + table(4, 5, left, partner) + table(5, 6, right, partner)
     t_last = table(6, 7, opp, partner)
 
+    lo, hi = pl.ds(0, half), pl.ds(half, half)
+
     def own(j):
-        return [
-            rcopy(xall.at[j, me], xall.at[j, me], as_sem.at[0, j], ar_sem.at[0, j], right),
-            rcopy(xall.at[j, me], xall.at[j, me], as_sem.at[1, j], ar_sem.at[1, j], left),
-            rcopy(xall.at[j, me], xall.at[j, me], as_sem.at[2, j], ar_sem.at[4, j], partner),
-        ]
-
-    lo, hi = pl.ds(0, half), pl.ds(half, half)
+        sends = ((lo, 0, 0, right), (hi, 1, 1, left), (hi, 8, 8, right), (lo, 9, 9, left))
+        return [
+            rcopy(xall.at[j, me, at], xall.at[j, me, at], as_sem.at[i, j], ar_sem.at[r, j], dev)
+            for at, i, r, dev in sends
+        ] + [rcopy(xall.at[j, me], xall.at[j, me], as_sem.at[2, j], ar_sem.at[4, j], partner)]
 
     def forward(j):
         return [
             rcopy(xall.at[j, left, lo], xall.at[j, left, lo], as_sem.at[3, j], ar_sem.at[2, j], right),
             rcopy(xall.at[j, right, hi], xall.at[j, right, hi], as_sem.at[4, j], ar_sem.at[3, j], left),
-            rcopy(xall.at[j, left], xall.at[j, left], as_sem.at[5, j], ar_sem.at[5, j], partner),
-            rcopy(xall.at[j, right], xall.at[j, right], as_sem.at[6, j], ar_sem.at[6, j], partner),
         ]
 
     def across(j):
-        return [rcopy(xall.at[j, opp], xall.at[j, opp], as_sem.at[7, j], ar_sem.at[7, j], partner)]
+        return [
+            rcopy(xall.at[j, s], xall.at[j, s], as_sem.at[i, j], ar_sem.at[i, j], partner)
+            for i, s in ((5, left), (6, right), (7, opp))
+        ]
 
     def send_own(j):
         xload(j).wait()
         go(own(j))
 
     def step_a(j):
-        got(xall.at[j, left], ar_sem.at[0, j])
-        got(xall.at[j, right], ar_sem.at[1, j])
+        got(xall.at[j, left, lo], ar_sem.at[0, j])
+        got(xall.at[j, right, hi], ar_sem.at[1, j])
         go(forward(j))
         if j + AHEAD < chunks:
             send_own(j + AHEAD)
 
     def step_b(j):
+        got(xall.at[j, left, hi], ar_sem.at[8, j])
+        got(xall.at[j, right, lo], ar_sem.at[9, j])
         got(xall.at[j, opp, lo], ar_sem.at[2, j])
         got(xall.at[j, opp, hi], ar_sem.at[3, j])
         go(across(j))
@@ -205,7 +208,7 @@
         lax.fori_loop(0, experts // STEP, pair, 0)
 
     def within(j):
-        return [(at, f(k)) for at, f, k in ((1, A, j + 2), (1, B, j + 1)) if k < chunks]
+        return [(at, f(k)) for at, f, k in ((0, A, j + 2), (1, B, j + 1)) if k < chunks]
 
     for g, js in enumerate(GROUPS):
         for i, j in enumerate(js):
@@ -370,8 +373,8 @@
                 dma((chunks,)),
                 dma((2, 7)),
                 dma((2, 8)),
-                dma((8, chunks)),
-                dma((8, chunks)),
+                dma((10, chunks)),
+                dma((10, chunks)),
                 dma((7, chunks)),
                 dma((7, chunks)),
             ],

time: 97 us -> 97.5 us (level)
  no operation moved by 1% of the time
where the time goes in v8:
time: 97.5 us; the launch traced here: 97.3 us
  Pallas kernels  95 us (97%)
  local copies, waits for them, and re-layouts  2.3 us (2%)
    pallas_call x1, Pallas kernels, local(): pl.pallas_call(functools.partial(kernel, n, slots, width), out_shape=jax....  95 us
    unnamed x1, local copies, waits for them, and re-layouts  2.3 us

profile of v8, /device:TPU:112, one launch (start us, length us, event | category | flops | bytes accessed | tf_op | source)
XLA Modules:
  0.0 97.3 jit_solution(10508930444894958884)
XLA Ops:
  0.0 95.0 %moe.1 = bf16[256,2048]{1,0:T(8,128)(2,1)} custom-call(bf16[256,2048]{1,0:T(8,128)(2,1)} %bitcast.12, s32[8,256]{1,0:T(8,128)} %bitcast.13, s32[8,256]{1,0:T(8,128)} %bitcast.14, f32[8,256]{1,0:T(8,128)} %bitcast.15, bf16[8,2048,1024]{2,1,0:T(8,128)(2,1)} %wg_hbm.1, bf16[8,2048,1024]{2,1,0:T(8,128)(2,1)} %wu_hbm.1, bf16[8,1024,2048]{2,1,0:T(8,128)(2,1)} %wd_hbm.1), custom_call_target="tpu_custom_call" | custom-call | flops 32212254720 | bytes 100663296 | tf_op jit(solution)/shard_map/moe/pallas_call | solution.py:348
  95.0 2.3 %copy.9 = bf16[1,1,256,2048]{3,2,1,0:T(8,128)(2,1)} copy(bf16[1,1,256,2048]{3,2,1,0:T(8,128)(2,1)} %bitcast.11) | data formatting | bytes 2097152
